TPU v7x, 32 devices: a whole 2x2x4 slice. The times are simulated.
32 devices in a mesh: grp: 4 (over z), ctx: 2 (over y), wid: 4 (over x, core).
Axes of the slice: x: 2, y: 2, z: 4, core: 2. Of those that a mesh axis runs over, the one named last changes fastest.
Arguments:
- query: bfloat16 [256, 64, 128], P(None, 'wid'), may hold values from -64 to 64
- keys: bfloat16 [4, 512, 8, 128], P(None, ('grp', 'ctx'), 'wid'), may hold values from -64 to 64
- values: bfloat16 [4, 512, 8, 128], P(None, ('grp', 'ctx'), 'wid'), may hold values from -6 to 6
- lengths: int32 [4, 8], replicated, may hold values from 32 to 64
- query_pos: int32 [256], replicated, may hold values from 128 to 511
- resid: bfloat16 [256, 5120], P('wid', ('grp', 'ctx')), may hold values from -1.1953125 to 1.1953125
- out_weight: bfloat16 [8192, 5120], P('wid', ('grp', 'ctx')), may hold values from -0.0625 to 0.0625
- enc_weight: bfloat16 [5120, 24576], P('wid', ('grp', 'ctx')), may hold values from -0.078125 to 0.078125
- enc_bias: float32 [24576], P(('grp', 'ctx')), may hold values from -3 to 3
- dec_weight: bfloat16 [24576, 5120], P(('grp', 'ctx'), 'wid'), may hold values from -0.078125 to 0.078125
- dec_bias: float32 [5120], P('wid'), may hold values from -3 to 3
Outputs:
- layer_out: bfloat16 [256, 5120], P('wid', ('grp', 'ctx'))
- enc_grad: bfloat16 [5120, 24576], P('wid', ('grp', 'ctx'))
- enc_bias_grad: float32 [24576], P(('grp', 'ctx'))
- dec_grad: bfloat16 [24576, 5120], P(('grp', 'ctx'), 'wid')
- dec_bias_grad: float32 [5120], P('wid')
Inputs may be any that keep to these rules, and one draw needn't show every extreme that they name: `lengths`: live slots of a shard are its first ones.
All inputs are finite; a program needn't handle non-finite values.
Results may differ from a plain program's by a relative error of at most 0.024.
Values may be sent and summed in bfloat16 or wider, within the bound.
A program may use at most 128 MiB of HBM per device.

v0:
```python
import jax
import jax.numpy as jnp
from jax import lax
from jax.sharding import PartitionSpec as P

HD = 128


def body(
    query,
    keys,
    values,
    lengths,
    query_pos,
    resid,
    out_weight,
    enc_weight,
    enc_bias,
    dec_weight,
    dec_bias,
):
    seq_count, slot_count, kv_local, head_dim = keys.shape
    row_count = query.shape[0]
    heads_local = query.shape[1]
    group_size = heads_local // kv_local
    rows_each = row_count // seq_count
    shard_pos = lax.axis_index(("grp", "ctx"))
    shard_ids = jnp.arange(lengths.shape[1], dtype=jnp.int32)
    offset = jnp.sum(jnp.where(shard_ids[None, :] < shard_pos, lengths, 0), axis=1)
    live_count = jnp.sum(jnp.where(shard_ids[None, :] == shard_pos, lengths, 0), axis=1)
    slot_ids = jnp.arange(slot_count, dtype=jnp.int32)
    key_pos = offset[:, None] + slot_ids[None, :]
    live_slot = slot_ids[None, :] < live_count[:, None]
    row_position = query_pos.reshape(seq_count, rows_each)
    visible = live_slot[:, None, :] & (key_pos[:, None, :] <= row_position[:, :, None])
    visible_mask = visible[:, :, None, None, :]
    q_view = query.reshape(seq_count, rows_each, kv_local, group_size, head_dim)
    scores = jnp.einsum(
        "srkgd,sjkd->srkgj", q_view, keys, preferred_element_type=jnp.float32
    ) * HD ** (-0.5)
    local_peak = jnp.max(jnp.where(visible_mask, scores, -1e30), axis=-1)
    peak = lax.pmax(local_peak, ("grp", "ctx"))
    weights = jnp.where(visible_mask, jnp.exp(scores - peak[..., None]), 0.0)
    weight_sum = jnp.sum(weights, axis=-1)
    weights_low = weights.astype(jnp.bfloat16)
    weighted = jnp.einsum(
        "srkgj,sjkd->srkgd", weights_low, values, preferred_element_type=jnp.float32
    )
    weight_sum, weighted = (weight_sum, weighted)
    weight_sum, weighted = lax.psum((weight_sum, weighted), ("grp", "ctx"))
    attention = (weighted / weight_sum[..., None]).astype(jnp.bfloat16)
    attention = attention.reshape(row_count, heads_local * head_dim)
    projected = jnp.dot(attention, out_weight, preferred_element_type=jnp.float32)
    mixed = lax.psum_scatter(
        projected.astype(jnp.bfloat16), "wid", scatter_dimension=0, tiled=True
    ).astype(jnp.float32)
    layer_out = (mixed + resid.astype(jnp.float32)).astype(jnp.bfloat16)
    wide_rows = lax.all_gather(layer_out, ("grp", "ctx"), axis=1, tiled=True)
    block = lax.all_to_all(wide_rows, "wid", split_axis=1, concat_axis=0, tiled=True)
    enc_part = jnp.dot(block, enc_weight, preferred_element_type=jnp.float32)
    preact = lax.psum(enc_part.astype(jnp.bfloat16), "wid").astype(jnp.float32) + enc_bias
    latents = (jax.nn.softplus(4.0 * preact) * 0.25).astype(jnp.bfloat16)
    row_scale = row_count ** (-0.5)
    recon = lax.psum_scatter(
        jnp.dot(latents, dec_weight, preferred_element_type=jnp.float32),
        ("grp", "ctx"),
        scatter_dimension=0,
        tiled=True,
    )
    piece_len = recon.shape[0]
    target = lax.dynamic_slice_in_dim(block, shard_pos * piece_len, piece_len, 0).astype(
        jnp.float32
    )
    scaled_error = ((recon + dec_bias - target) * row_scale).astype(jnp.bfloat16)
    error_all = lax.all_gather(scaled_error, ("grp", "ctx"), axis=0, tiled=True)
    dec_bias_grad = jnp.sum(error_all, axis=0, dtype=jnp.float32)
    latent_part = lax.dot_general(
        error_all, dec_weight, (((1,), (1,)), ((), ())), preferred_element_type=jnp.float32
    )
    dec_grad = lax.dot_general(
        latents, error_all, (((0,), (0,)), ((), ())), preferred_element_type=jnp.float32
    )
    latent_grad = lax.psum(latent_part.astype(jnp.bfloat16), "wid").astype(jnp.float32)
    preact_grad = (latent_grad * jax.nn.sigmoid(4.0 * preact)).astype(jnp.bfloat16)
    enc_grad = lax.dot_general(
        block, preact_grad, (((0,), (0,)), ((), ())), preferred_element_type=jnp.float32
    ).astype(jnp.bfloat16)
    enc_bias_grad = jnp.sum(preact_grad, axis=0, dtype=jnp.float32)
    return (layer_out, enc_grad, enc_bias_grad, dec_grad.astype(jnp.bfloat16), dec_bias_grad)


def solution(mesh):
    placed = (
        P(None, "wid", None),
        P(None, ("grp", "ctx"), "wid", None),
        P(None, ("grp", "ctx"), "wid", None),
        P(),
        P(),
        P("wid", ("grp", "ctx")),
        P("wid", ("grp", "ctx")),
        P("wid", ("grp", "ctx")),
        P(("grp", "ctx")),
        P(("grp", "ctx"), "wid"),
        P("wid"),
    )
    return jax.shard_map(
        body,
        mesh=mesh,
        in_specs=placed,
        out_specs=(
            P("wid", ("grp", "ctx")),
            P("wid", ("grp", "ctx")),
            P(("grp", "ctx")),
            P(("grp", "ctx"), "wid"),
            P("wid"),
        ),
        check_vma=False,
    )
```

profile of v0, /device:TPU:0, one launch (start us, length us, event | category | flops | bytes accessed | tf_op | source)
XLA Modules:
  0.0 456.0 jit_solution(1669517848478432027)
XLA Ops:
  7.2 0.0 copy-start
  7.2 0.0 all-reduce.4.cloned.1.call-start
  7.2 0.9 le.20
  8.1 0.8 select_reduce_fusion.1
  9.0 0.1 iota_add_fusion
  9.0 0.1 iota_compare_fusion
  9.1 0.1 compare_and_fusion
  9.3 3.8 fusion.2
  13.0 0.0 copy-start.3
  13.0 39.0 %pmax.7 = f32[4,64,2,8]{1,3,2,0:T(8,128)S(1)} all-reduce(f32[4,64,2,8]{1,3,2,0:T(8,128)S(1)} %get-tuple-element.11), channel_id=1, replica_groups=mesh['grp'=4,'ctx'=2,'wid'=4] {'grp','ctx'}, use_global_device_ids=true, to_apply=%region_3.4 | all-reduce | flops 4096 | bytes 32768 | tf_op jit(solution)/shard_map/pmax | solution.py:42
  52.0 3.2 fusion.5
  55.3 2.4 copy.29
  57.7 0.0 copy-done.3
  57.7 3.0 convolution_bitcast_fusion
  60.6 0.0 all-reduce.4.cloned.1.call-update
  60.7 0.0 reduce-scatter.3.cloned.1.call-start
  60.7 34.2 %psum.29 = f32[4,64,2,8]{1,3,2,0:T(8,128)S(1)} all-reduce(f32[4,64,2,8]{1,3,2,0:T(8,128)S(1)} %get-tuple-element.9), channel_id=1, replica_groups=mesh['grp'=4,'ctx'=2,'wid'=4] {'grp','ctx'}, use_global_device_ids=true, to_apply=%region_6.7 | all-reduce | flops 4096 | bytes 32768 | tf_op jit(solution)/shard_map/psum | solution.py:50
  94.9 0.1 copy.31
  95.0 65.7 %all-reduce.4.cloned.1.call-done = f32[4,64,2,8,128]{4,3,1,2,0:T(8,128)} async-done(((f32[4,64,2,8,128]{4,3,1,2,0:T(8,128)}), f32[4,64,2,8,128]{4,3,1,2,0:T(8,128)}) %all-reduce.4.cloned.1.call-update) | async-done | bytes 2097168 | tf_op jit(solution)/shard_map/psum | solution.py:50
  160.8 1.9 divide_convert_fusion
  162.7 1.2 copy.32
  163.9 0.0 copy-start.4
  163.9 2.3 reshape.71
  166.2 0.0 copy-done
  166.2 2.9 convolution_convert_fusion.4
  169.1 0.0 reduce-scatter.3.cloned.1.call-update
  169.1 0.0 all-reduce.6.cloned.1.call-start
  169.2 19.8 %reduce-scatter.3.cloned.1.call-done = bf16[64,640]{1,0:T(8,128)(2,1)} async-done(((bf16[256,640]{1,0:T(8,128)(2,1)}), bf16[64,640]{1,0:T(8,128)(2,1)}) %reduce-scatter.3.cloned.1.call-update) | async-done | bytes 81936 | tf_op jit(solution)/shard_map/reduce_scatter | solution.py:54
  189.0 0.0 copy-done.4
  189.0 0.9 add_convert_fusion
  189.9 0.0 copy-start.2
  189.9 32.1 %all_gather.6 = bf16[64,5120]{1,0:T(8,128)(2,1)S(1)} all-gather(bf16[64,640]{1,0:T(8,128)(2,1)S(1)} %add_convert_fusion), channel_id=1, replica_groups=mesh['grp'=4,'ctx'=2,'wid'=4] {'grp','ctx'}, dimensions={1}, use_global_device_ids=true | all-gather | bytes 737280 | tf_op jit(solution)/shard_map/all_gather | solution.py:58
  222.1 12.6 %all_to_all.19 = bf16[64,4,1280]{2,0,1:T(8,128)(2,1)S(1)} all-to-all(bf16[64,4,1280]{2,0,1:T(8,128)(2,1)S(1)} %bitcast.41), channel_id=1, replica_groups=mesh['grp'=4,'ctx'=2,'wid'=4] {'wid'}, dimensions={1} | all-to-all | bytes 1310720 | tf_op jit(solution)/shard_map/all_to_all | solution.py:59
  234.7 0.0 copy-start.5
  234.7 6.6 %convolution_convert_fusion.3 = bf16[256,3072]{1,0:T(8,128)(2,1)} fusion(bf16[256,1280]{1,0:T(8,128)(2,1)S(1)} %bitcast.38, bf16[1280,3072]{1,0:T(8,128)(2,1)} %param.18), kind=kOutput, calls=%fused_computation.4 | convolution fusion | flops 2014052352 | bytes 10092544 | tf_op jit(solution)/shard_map/dot_general | solution.py:60
  241.3 0.0 copy-done.2
  241.3 0.0 all-reduce.6.cloned.1.call-update
  241.4 0.0 copy-start.6
  241.4 0.0 reduce-scatter.5.cloned.1.call-start
  241.4 42.7 %all-reduce.6.cloned.1.call-done = bf16[256,3072]{1,0:T(8,128)(2,1)} async-done(((bf16[256,3072]{1,0:T(8,128)(2,1)}), bf16[256,3072]{1,0:T(8,128)(2,1)}) %all-reduce.6.cloned.1.call-update) | async-done | bytes 1572880 | tf_op jit(solution)/shard_map/psum | solution.py:61
  284.1 0.0 copy-done.5
  284.1 8.8 %fusion.12 = f32[256,1280]{1,0:T(8,128)} fusion(bf16[3072,1280]{1,0:T(8,128)(2,1)} %param.20, bf16[256,3072]{1,0:T(8,128)(2,1)} %all-reduce.6.cloned.1.call-done, f32[3072]{0:T(1024)S(1)} %copy-done.5), kind=kOutput, calls=%fused_computation.35 | convolution fusion | flops 2021916672 | bytes 10760192 | tf_op jit(solution)/shard_map/dot_general | solution.py:65
  292.9 0.0 reduce-scatter.5.cloned.1.call-update
  293.0 0.0 all-reduce.8.cloned.1.call-start
  293.0 65.3 %reduce-scatter.5.cloned.1.call-done = f32[32,1280]{1,0:T(8,128)} async-done(((f32[256,1280]{1,0:T(8,128)}), f32[32,1280]{1,0:T(8,128)}) %reduce-scatter.5.cloned.1.call-update) | async-done | bytes 163856 | tf_op jit(solution)/shard_map/reduce_scatter | solution.py:64
  358.3 0.0 copy-done.6
  358.3 0.9 multiply_convert_fusion.1
  359.2 32.1 %all_gather.7 = bf16[256,1280]{1,0:T(8,128)(2,1)S(1)} all-gather(bf16[32,1280]{1,0:T(8,128)(2,1)S(1)} %multiply_convert_fusion.1), channel_id=1, replica_groups=mesh['grp'=4,'ctx'=2,'wid'=4] {'grp','ctx'}, dimensions={0}, use_global_device_ids=true | all-gather | bytes 737280 | tf_op jit(solution)/shard_map/all_gather | solution.py:75
  391.4 0.0 copy-start.1
  391.4 0.8 copy-done.1
  392.2 6.6 %convolution_convert_fusion.2 = bf16[256,3072]{1,0:T(8,128)(2,1)} fusion(bf16[256,1280]{1,0:T(8,128)(2,1)S(1)} %all_gather.7, bf16[3072,1280]{1,0:T(8,128)(2,1)} %param.20), kind=kOutput, calls=%fused_computation.3 | convolution fusion | flops 2014052352 | bytes 10092544 | tf_op jit(solution)/shard_map/dot_general | solution.py:77
  398.8 0.0 all-reduce.8.cloned.1.call-update
  398.8 1.8 convert_reduce_fusion.1
  400.6 9.0 %convolution_convert_fusion = bf16[3072,1280]{1,0:T(8,128)(2,1)} fusion(bf16[256,1280]{1,0:T(8,128)(2,1)} %copy-done.1, bf16[256,3072]{1,0:T(8,128)(2,1)} %all-reduce.6.cloned.1.call-done, f32[3072]{0:T(1024)S(1)} %copy-done.5), kind=kOutput, calls=%fused_computation | convolution fusion | flops 2025848832 | bytes 10104832 | tf_op jit(solution)/shard_map/dot_general | solution.py:80
  409.6 30.8 %all-reduce.8.cloned.1.call-done = bf16[256,3072]{1,0:T(8,128)(2,1)} async-done(((bf16[256,3072]{1,0:T(8,128)(2,1)}), bf16[256,3072]{1,0:T(8,128)(2,1)}) %all-reduce.8.cloned.1.call-update) | async-done | bytes 1572880 | tf_op jit(solution)/shard_map/psum | solution.py:83
  440.4 3.6 convert_reduce_fusion
  444.0 5.5 %convolution_convert_fusion.1 = bf16[1280,3072]{1,0:T(8,128)(2,1)} fusion(bf16[256,1280]{1,0:T(8,128)(2,1)S(1)} %bitcast.40, bf16[256,3072]{1,0:T(8,128)(2,1)S(1)} %get-tuple-element.8), kind=kOutput, calls=%fused_computation.1 | convolution fusion | flops 2017198080 | bytes 10092544 | tf_op jit(solution)/shard_map/dot_general | solution.py:85
  (2 shorter events, 0.0 us)
Async XLA Ops:
  7.2 159.0 %copy-start = (bf16[2048,640]{1,0:T(8,128)(2,1)S(1)}, bf16[2048,640]{1,0:T(8,128)(2,1)}, u32[]{:S(2)}) copy-start(bf16[2048,640]{1,0:T(8,128)(2,1)} %param.17) | copy-start | bytes 7864324
  7.2 153.6 %all-reduce.4.cloned.1.call-start = ((), (), s32[]{:S(2)}) async-start(), calls=%async_computation.3 | async-start | bytes 4194304 | tf_op jit(solution)/shard_map/psum | solution.py:50
  13.0 44.6 %copy-start.3 = (bf16[4,64,2,128]{3,2,1,0:T(2,128)(2,1)S(1)}, bf16[4,64,2,128]{3,2,1,0:T(2,128)(2,1)}, u32[]{:S(2)}) copy-start(bf16[4,64,2,128]{3,2,1,0:T(2,128)(2,1)} %param.13) | copy-start | bytes 393220
  60.7 128.4 %reduce-scatter.3.cloned.1.call-start = ((), (), s32[]{:S(2)}) async-start(), calls=%async_computation.4 | async-start | bytes 409600 | tf_op jit(solution)/shard_map/reduce_scatter | solution.py:54
  163.9 25.1 %copy-start.4 = (bf16[64,640]{1,0:T(8,128)(2,1)S(1)}, bf16[64,640]{1,0:T(8,128)(2,1)}, u32[]{:S(2)}) copy-start(bf16[64,640]{1,0:T(8,128)(2,1)} %param.16) | copy-start | bytes 245764
  169.1 114.9 %all-reduce.6.cloned.1.call-start = ((), (), s32[]{:S(2)}) async-start(), calls=%async_computation.5 | async-start | bytes 3145728 | tf_op jit(solution)/shard_map/psum | solution.py:61
  189.9 51.4 %copy-start.2 = (bf16[64,640]{1,0:T(8,128)(2,1)}, bf16[64,640]{1,0:T(8,128)(2,1)S(1)}, u32[]{:S(2)}) copy-start(bf16[64,640]{1,0:T(8,128)(2,1)S(1)} %add_convert_fusion) | copy-start | bytes 245764
  234.7 49.3 %copy-start.5 = (f32[3072]{0:T(1024)S(1)}, f32[3072]{0:T(1024)}, u32[]{:S(2)}) copy-start(f32[3072]{0:T(1024)} %param.19) | copy-start | bytes 36868
  241.4 116.9 %copy-start.6 = (f32[1280]{0:T(1024)S(1)}, f32[1280]{0:T(1024)}, u32[]{:S(2)}) copy-start(f32[1280]{0:T(1024)} %param.21) | copy-start | bytes 15364
  241.4 116.9 %reduce-scatter.5.cloned.1.call-start = ((), (), s32[]{:S(2)}) async-start(), calls=%async_computation.6 | async-start | bytes 1474560 | tf_op jit(solution)/shard_map/reduce_scatter | solution.py:64
  293.0 147.5 %all-reduce.8.cloned.1.call-start = ((), (), s32[]{:S(2)}) async-start(), calls=%async_computation.7 | async-start | bytes 3145728 | tf_op jit(solution)/shard_map/psum | solution.py:83
  391.4 0.8 copy-start.1
Sparse Core Ops, SparseCore 0:
  60.8 99.9 all-reduce.3
  169.3 19.6 reduce-scatter.2
  241.5 42.5 all-reduce.5
  293.1 65.1 reduce-scatter.4
  398.9 41.4 all-reduce.7
where the time goes:
time: 457 us; the launch traced here: 456 us
  waiting for transfers between devices  224 us (49%)
  blocking collectives  150 us (33%)
  matrix products  46.2 us (10%)
  between operations  13.9 us (3%)
  other arithmetic  13.5 us (3%)
  local copies, waits for them, and re-layouts  7.82 us (2%)
    psum x1, waiting for transfers between devices, body(): weight_sum, weighted = lax.psum((weight_sum, weighted), ('grp', 'ctx'))  65.7 us
    reduce_scatter x1, waiting for transfers between devices, body(): lax.psum_scatter(jnp.dot(latents, dec_weight, preferred_element_type=jnp....  65.3 us
    psum x1, waiting for transfers between devices, body(): lax.psum(enc_part.astype(jnp.bfloat16), 'wid').astype(jnp.float32)  42.7 us
    pmax x1, blocking collectives, body(): peak = lax.pmax(local_peak, ('grp', 'ctx'))  39 us
    psum x1, blocking collectives, body(): weight_sum, weighted = lax.psum((weight_sum, weighted), ('grp', 'ctx'))  34.2 us
    all_gather x1, blocking collectives, body(): wide_rows = lax.all_gather(layer_out, ('grp', 'ctx'), axis=1, tiled=True)  32.1 us
    all_gather x1, blocking collectives, body(): error_all = lax.all_gather(scaled_error, ('grp', 'ctx'), axis=0, tiled=True)  32.1 us
    psum x1, waiting for transfers between devices, body(): lax.psum(latent_part.astype(jnp.bfloat16), 'wid').astype(jnp.float32)  30.8 us
  transfers between devices with their start and end apart: 5, of which 5 were waited for; matrix products, arithmetic and copies ran while one was open for 2% of the time, Pallas kernels for 0%

commit v1 on v0

--- a/solution.py
+++ b/solution.py
@@ -80,7 +80,9 @@
     dec_grad = lax.dot_general(
         latents, error_all, (((0,), (0,)), ((), ())), preferred_element_type=jnp.float32
     )
-    latent_grad = lax.psum(latent_part.astype(jnp.bfloat16), "wid").astype(jnp.float32)
+    latent_grad = jnp.sum(lax.all_gather(latent_part.astype(jnp.bfloat16), "wid"), axis=0).astype(
+        jnp.float32
+    )
     preact_grad = (latent_grad * jax.nn.sigmoid(4.0 * preact)).astype(jnp.bfloat16)
     enc_grad = lax.dot_general(
         block, preact_grad, (((0,), (0,)), ((), ())), preferred_element_type=jnp.float32

time: 457 us -> 466 us (1.020)
  other arithmetic: 13.5 us -> 19 us
    all_gather x0 -> x1, waiting for transfers between devices: none -> 33.9 us  [body(): lax.all_gather(latent_part.astype(jnp.bfloat16), 'wid')]
    psum x1 -> x0, waiting for transfers between devices: 30.8 us -> none  [body(): lax.psum(latent_part.astype(jnp.bfloat16), 'wid').astype(jnp.float32)]
    reduce_sum x0 -> x1, other arithmetic: none -> 5.52 us  [body(): jnp.sum(lax.all_gather(latent_part.astype(jnp.bfloat16), 'wid'), axis=0)]
where the time goes in v1:
time: 466 us; the launch traced here: 465 us
  waiting for transfers between devices  227 us (49%)
  blocking collectives  150 us (32%)
  matrix products  46.5 us (10%)
  other arithmetic  19 us (4%)
  between operations  13.9 us (3%)
  local copies, waits for them, and re-layouts  7.88 us (2%)
    psum x1, waiting for transfers between devices, body(): weight_sum, weighted = lax.psum((weight_sum, weighted), ('grp', 'ctx'))  65.7 us
    reduce_scatter x1, waiting for transfers between devices, body(): lax.psum_scatter(jnp.dot(latents, dec_weight, preferred_element_type=jnp....  65.2 us
    psum x1, waiting for transfers between devices, body(): lax.psum(enc_part.astype(jnp.bfloat16), 'wid').astype(jnp.float32)  42.7 us
    pmax x1, blocking collectives, body(): peak = lax.pmax(local_peak, ('grp', 'ctx'))  39 us
    psum x1, blocking collectives, body(): weight_sum, weighted = lax.psum((weight_sum, weighted), ('grp', 'ctx'))  34.2 us
    all_gather x1, waiting for transfers between devices, body(): lax.all_gather(latent_part.astype(jnp.bfloat16), 'wid')  33.9 us
    all_gather x1, blocking collectives, body(): error_all = lax.all_gather(scaled_error, ('grp', 'ctx'), axis=0, tiled=True)  32.2 us
    all_gather x1, blocking collectives, body(): wide_rows = lax.all_gather(layer_out, ('grp', 'ctx'), axis=1, tiled=True)  32.1 us
  transfers between devices with their start and end apart: 5, of which 5 were waited for; matrix products, arithmetic and copies ran while one was open for 2% of the time, Pallas kernels for 0%

profile of v1, /device:TPU:0, one launch (start us, length us, event | category | flops | bytes accessed | tf_op | source)
XLA Modules:
  0.0 465.0 jit_solution(13542333577863821163)
XLA Ops:
  7.2 0.0 copy-start
  7.2 0.0 all-reduce.3.cloned.1.call-start
  7.2 0.9 le.20
  8.1 0.8 select_reduce_fusion.1
  9.0 0.1 iota_add_fusion
  9.0 0.1 iota_compare_fusion
  9.1 0.1 compare_and_fusion
  9.3 3.8 fusion.2
  13.0 0.0 copy-start.3
  13.0 39.0 %pmax.7 = f32[4,64,2,8]{1,3,2,0:T(8,128)S(1)} all-reduce(f32[4,64,2,8]{1,3,2,0:T(8,128)S(1)} %get-tuple-element.11), channel_id=1, replica_groups=mesh['grp'=4,'ctx'=2,'wid'=4] {'grp','ctx'}, use_global_device_ids=true, to_apply=%region_3.4 | all-reduce | flops 4096 | bytes 32768 | tf_op jit(solution)/shard_map/pmax | solution.py:42
  52.0 3.2 fusion.5
  55.3 2.4 copy.29
  57.7 0.0 copy-done.3
  57.7 3.0 convolution_bitcast_fusion
  60.6 0.0 all-reduce.3.cloned.1.call-update
  60.7 0.0 reduce-scatter.3.cloned.1.call-start
  60.7 34.2 %psum.22 = f32[4,64,2,8]{1,3,2,0:T(8,128)S(1)} all-reduce(f32[4,64,2,8]{1,3,2,0:T(8,128)S(1)} %get-tuple-element.9), channel_id=1, replica_groups=mesh['grp'=4,'ctx'=2,'wid'=4] {'grp','ctx'}, use_global_device_ids=true, to_apply=%region_6.7 | all-reduce | flops 4096 | bytes 32768 | tf_op jit(solution)/shard_map/psum | solution.py:50
  94.9 0.1 copy.31
  95.0 65.7 %all-reduce.3.cloned.1.call-done = f32[4,64,2,8,128]{4,3,1,2,0:T(8,128)} async-done(((f32[4,64,2,8,128]{4,3,1,2,0:T(8,128)}), f32[4,64,2,8,128]{4,3,1,2,0:T(8,128)}) %all-reduce.3.cloned.1.call-update) | async-done | bytes 2097168 | tf_op jit(solution)/shard_map/psum | solution.py:50
  160.8 1.9 divide_convert_fusion
  162.7 1.2 copy.32
  163.9 0.0 copy-start.4
  163.9 2.3 reshape.71
  166.2 0.0 copy-done
  166.2 2.9 convolution_convert_fusion.4
  169.1 0.0 reduce-scatter.3.cloned.1.call-update
  169.1 0.0 all-reduce.5.cloned.1.call-start
  169.2 19.8 %reduce-scatter.3.cloned.1.call-done = bf16[64,640]{1,0:T(8,128)(2,1)} async-done(((bf16[256,640]{1,0:T(8,128)(2,1)}), bf16[64,640]{1,0:T(8,128)(2,1)}) %reduce-scatter.3.cloned.1.call-update) | async-done | bytes 81936 | tf_op jit(solution)/shard_map/reduce_scatter | solution.py:54
  189.0 0.0 copy-done.4
  189.0 0.9 add_convert_fusion
  189.9 0.0 copy-start.2
  189.9 32.1 %all_gather.12 = bf16[64,5120]{1,0:T(8,128)(2,1)S(1)} all-gather(bf16[64,640]{1,0:T(8,128)(2,1)S(1)} %add_convert_fusion), channel_id=1, replica_groups=mesh['grp'=4,'ctx'=2,'wid'=4] {'grp','ctx'}, dimensions={1}, use_global_device_ids=true | all-gather | bytes 737280 | tf_op jit(solution)/shard_map/all_gather | solution.py:58
  222.1 12.6 %all_to_all.19 = bf16[64,4,1280]{2,0,1:T(8,128)(2,1)S(1)} all-to-all(bf16[64,4,1280]{2,0,1:T(8,128)(2,1)S(1)} %bitcast.43), channel_id=1, replica_groups=mesh['grp'=4,'ctx'=2,'wid'=4] {'wid'}, dimensions={1} | all-to-all | bytes 1310720 | tf_op jit(solution)/shard_map/all_to_all | solution.py:59
  234.7 0.0 copy-start.5
  234.7 6.6 %convolution_convert_fusion.3 = bf16[256,3072]{1,0:T(8,128)(2,1)} fusion(bf16[256,1280]{1,0:T(8,128)(2,1)S(1)} %bitcast.40, bf16[1280,3072]{1,0:T(8,128)(2,1)} %param.18), kind=kOutput, calls=%fused_computation.4 | convolution fusion | flops 2014052352 | bytes 10092544 | tf_op jit(solution)/shard_map/dot_general | solution.py:60
  241.3 0.0 copy-done.2
  241.3 0.0 all-reduce.5.cloned.1.call-update
  241.4 0.0 copy-start.6
  241.4 0.0 reduce-scatter.5.cloned.1.call-start
  241.4 42.7 %all-reduce.5.cloned.1.call-done = bf16[256,3072]{1,0:T(8,128)(2,1)} async-done(((bf16[256,3072]{1,0:T(8,128)(2,1)}), bf16[256,3072]{1,0:T(8,128)(2,1)}) %all-reduce.5.cloned.1.call-update) | async-done | bytes 1572880 | tf_op jit(solution)/shard_map/psum | solution.py:61
  284.1 0.0 copy-done.5
  284.1 8.8 %fusion.12 = f32[256,1280]{1,0:T(8,128)} fusion(bf16[3072,1280]{1,0:T(8,128)(2,1)} %param.20, bf16[256,3072]{1,0:T(8,128)(2,1)} %all-reduce.5.cloned.1.call-done, f32[3072]{0:T(1024)S(1)} %copy-done.5), kind=kOutput, calls=%fused_computation.35 | convolution fusion | flops 2021916672 | bytes 10760192 | tf_op jit(solution)/shard_map/dot_general | solution.py:65
  292.9 0.0 reduce-scatter.5.cloned.1.call-update
  293.0 0.0 all-gather.3.cloned.1.call-start
  293.0 65.2 %reduce-scatter.5.cloned.1.call-done = f32[32,1280]{1,0:T(8,128)} async-done(((f32[256,1280]{1,0:T(8,128)}), f32[32,1280]{1,0:T(8,128)}) %reduce-scatter.5.cloned.1.call-update) | async-done | bytes 163856 | tf_op jit(solution)/shard_map/reduce_scatter | solution.py:64
  358.2 0.0 copy-done.6
  358.2 0.9 multiply_convert_fusion.1
  359.1 32.2 %all_gather.13 = bf16[256,1280]{1,0:T(8,128)(2,1)S(1)} all-gather(bf16[32,1280]{1,0:T(8,128)(2,1)S(1)} %multiply_convert_fusion.1), channel_id=1, replica_groups=mesh['grp'=4,'ctx'=2,'wid'=4] {'grp','ctx'}, dimensions={0}, use_global_device_ids=true | all-gather | bytes 737280 | tf_op jit(solution)/shard_map/all_gather | solution.py:75
  391.3 0.0 copy-start.1
  391.3 0.9 copy-done.1
  392.2 6.6 %convolution_convert_fusion.2 = bf16[256,3072]{1,0:T(8,128)(2,1)} fusion(bf16[256,1280]{1,0:T(8,128)(2,1)S(1)} %all_gather.13, bf16[3072,1280]{1,0:T(8,128)(2,1)} %param.20), kind=kOutput, calls=%fused_computation.3 | convolution fusion | flops 2014052352 | bytes 10092544 | tf_op jit(solution)/shard_map/dot_general | solution.py:77
  398.8 0.0 all-gather.3.cloned.1.call-update
  398.8 1.8 convert_reduce_fusion.1
  400.6 9.4 %convolution_convert_fusion = bf16[3072,1280]{1,0:T(8,128)(2,1)} fusion(bf16[256,1280]{1,0:T(8,128)(2,1)} %copy-done.1, bf16[256,3072]{1,0:T(8,128)(2,1)} %all-reduce.5.cloned.1.call-done, f32[3072]{0:T(1024)S(1)} %copy-done.5), kind=kOutput, calls=%fused_computation | convolution fusion | flops 2025848832 | bytes 10104832 | tf_op jit(solution)/shard_map/dot_general | solution.py:80
  410.0 33.9 %all-gather.3.cloned.1.call-done = bf16[1024,3072]{1,0:T(8,128)(2,1)} async-done(((bf16[256,3072]{1,0:T(8,128)(2,1)}), bf16[1024,3072]{1,0:T(8,128)(2,1)}) %all-gather.3.cloned.1.call-update) | async-done | bytes 6291472 | tf_op jit(solution)/shard_map/all_gather | solution.py:83
  443.9 5.5 %reduce_sum.60 = bf16[256,3072]{1,0:T(8,128)(2,1)} reduce(bf16[4,256,3072]{2,1,0:T(8,128)(2,1)} %bitcast.39, bf16[]{:T(256)} %constant.36.clone.1), dimensions={0}, to_apply=%region_10.11 | reduce | flops 2359296 | bytes 7864322 | tf_op jit(solution)/shard_map/reduce_sum | solution.py:83
  449.4 3.6 convert_reduce_fusion
  453.0 5.5 %convolution_convert_fusion.1 = bf16[1280,3072]{1,0:T(8,128)(2,1)} fusion(bf16[256,1280]{1,0:T(8,128)(2,1)S(1)} %bitcast.42, bf16[256,3072]{1,0:T(8,128)(2,1)S(1)} %get-tuple-element.8), kind=kOutput, calls=%fused_computation.1 | convolution fusion | flops 2017198080 | bytes 10092544 | tf_op jit(solution)/shard_map/dot_general | solution.py:87
  (2 shorter events, 0.0 us)
Async XLA Ops:
  7.2 159.0 %copy-start = (bf16[2048,640]{1,0:T(8,128)(2,1)S(1)}, bf16[2048,640]{1,0:T(8,128)(2,1)}, u32[]{:S(2)}) copy-start(bf16[2048,640]{1,0:T(8,128)(2,1)} %param.17) | copy-start | bytes 7864324
  7.2 153.6 %all-reduce.3.cloned.1.call-start = ((), (), s32[]{:S(2)}) async-start(), calls=%async_computation.3 | async-start | bytes 4194304 | tf_op jit(solution)/shard_map/psum | solution.py:50
  13.0 44.6 %copy-start.3 = (bf16[4,64,2,128]{3,2,1,0:T(2,128)(2,1)S(1)}, bf16[4,64,2,128]{3,2,1,0:T(2,128)(2,1)}, u32[]{:S(2)}) copy-start(bf16[4,64,2,128]{3,2,1,0:T(2,128)(2,1)} %param.13) | copy-start | bytes 393220
  60.7 128.4 %reduce-scatter.3.cloned.1.call-start = ((), (), s32[]{:S(2)}) async-start(), calls=%async_computation.4 | async-start | bytes 409600 | tf_op jit(solution)/shard_map/reduce_scatter | solution.py:54
  163.9 25.1 %copy-start.4 = (bf16[64,640]{1,0:T(8,128)(2,1)S(1)}, bf16[64,640]{1,0:T(8,128)(2,1)}, u32[]{:S(2)}) copy-start(bf16[64,640]{1,0:T(8,128)(2,1)} %param.16) | copy-start | bytes 245764
  169.1 114.9 %all-reduce.5.cloned.1.call-start = ((), (), s32[]{:S(2)}) async-start(), calls=%async_computation.5 | async-start | bytes 3145728 | tf_op jit(solution)/shard_map/psum | solution.py:61
  189.9 51.4 %copy-start.2 = (bf16[64,640]{1,0:T(8,128)(2,1)}, bf16[64,640]{1,0:T(8,128)(2,1)S(1)}, u32[]{:S(2)}) copy-start(bf16[64,640]{1,0:T(8,128)(2,1)S(1)} %add_convert_fusion) | copy-start | bytes 245764
  234.7 49.3 %copy-start.5 = (f32[3072]{0:T(1024)S(1)}, f32[3072]{0:T(1024)}, u32[]{:S(2)}) copy-start(f32[3072]{0:T(1024)} %param.19) | copy-start | bytes 36868
  241.4 116.8 %copy-start.6 = (f32[1280]{0:T(1024)S(1)}, f32[1280]{0:T(1024)}, u32[]{:S(2)}) copy-start(f32[1280]{0:T(1024)} %param.21) | copy-start | bytes 15364
  241.4 116.8 %reduce-scatter.5.cloned.1.call-start = ((), (), s32[]{:S(2)}) async-start(), calls=%async_computation.6 | async-start | bytes 1474560 | tf_op jit(solution)/shard_map/reduce_scatter | solution.py:64
  293.0 151.0 %all-gather.3.cloned.1.call-start = ((), (), s32[]{:S(2)}) async-start(), calls=%async_computation.7 | async-start | bytes 7864320 | tf_op jit(solution)/shard_map/all_gather | solution.py:83
  391.3 0.9 copy-start.1
Sparse Core Ops, SparseCore 0:
  60.8 99.9 all-reduce.2
  169.3 19.6 reduce-scatter.2
  241.5 42.5 all-reduce.4
  293.1 65.0 reduce-scatter.4
  399.0 44.9 all-gather.2
